TPU v7x, 32 devices: a whole 2x2x4 slice. The times are simulated.
32 devices in a mesh: dp: 8 (over z, y), mp: 4 (over x, core).
Axes of the slice: x: 2, y: 2, z: 4, core: 2. Of those that a mesh axis runs over, the one named last changes fastest.
Arguments:
- image_tokens: bfloat16 [8, 192, 3072], P('dp'), may hold values from -6 to 6
- text_tokens: bfloat16 [8, 64, 3072], P('dp'), may hold values from -6 to 6
- null_prompt: bfloat16 [64, 3072], replicated, may hold values from -6 to 6
- drop_flags: int32 [8], P('dp'), may hold values 0 or 1
- time_index: int32 [8], P('dp'), may hold values from 0 to 31
- modulation: float32 [32, 3, 3072], replicated, may hold values from -3 to 3
- w_up: bfloat16 [3072, 12288], P('dp', 'mp'), may hold values from -0.109375 to 0.109375
- w_down: bfloat16 [12288, 3072], P('mp', 'dp'), may hold values from -0.0546875 to 0.0546875
- d_output: bfloat16 [8, 256, 3072], P('dp'), may hold values from -6 to 6
Outputs:
- block_out: bfloat16 [8, 256, 3072], P('dp')
- d_tokens: bfloat16 [8, 256, 3072], P('dp')
- grad_up: float32 [3072, 12288], P('dp', 'mp')
- grad_down: float32 [12288, 3072], P('mp', 'dp')
- grad_null: float32 [64, 3072], replicated
All inputs are finite; a program needn't handle non-finite values. No bound on the sum of `drop_flags` on one device may be relied on, other than what follows from the above.
Results may differ from a plain program's by a relative error of at most 0.017.
Values may be sent and summed in bfloat16 or wider, within the bound.
A program may use at most 128 MiB of HBM per device.

v0:
```python
import jax
import jax.numpy as jnp
from jax import lax
from jax.sharding import PartitionSpec as P

EPS = 1e-06


def gelu_tanh(values):
    return jax.nn.gelu(values, approximate=True)


def contract_rows(left, right):
    return lax.dot_general(
        left, right, (((0,), (0,)), ((), ())), preferred_element_type=jnp.float32
    )


def contract_cols(left, right):
    return lax.dot_general(
        left, right, (((1,), (1,)), ((), ())), preferred_element_type=jnp.float32
    )


def shards(
    image_tokens,
    text_tokens,
    null_prompt,
    drop_flags,
    time_index,
    modulation,
    w_up,
    w_down,
    d_output,
):
    dropped = drop_flags == 1
    text_in = jnp.where(dropped[:, None, None], null_prompt[None], text_tokens)
    joined = jnp.concatenate([text_in, image_tokens], axis=1)
    levels = jnp.arange(modulation.shape[0], dtype=jnp.int32)
    indicator_matrix = (time_index[:, None] == levels[None, :]).astype(jnp.float32)
    modulation_vectors = jnp.einsum(
        "yi,imr->ymr", indicator_matrix, modulation, precision=lax.Precision.HIGHEST
    )
    shift_modulation = modulation_vectors[:, 0][:, None]
    scale_mod = modulation_vectors[:, 1][:, None]
    gate_mod = modulation_vectors[:, 2][:, None]
    batch, length, width = joined.shape
    joined32 = joined.astype(jnp.float32)
    centred = joined32 - jnp.mean(joined32, axis=-1, keepdims=True)
    inv_std = lax.rsqrt(jnp.mean(centred * centred, axis=-1, keepdims=True) + EPS)
    normed = centred * inv_std
    mod_in = (normed * (1.0 + scale_mod) + shift_modulation).astype(jnp.bfloat16)
    flat_in = mod_in.reshape(batch * length, width)
    full_up, full_down = (
        lax.all_gather(w_up, "dp", axis=0, tiled=True),
        lax.all_gather(w_down, "dp", axis=1, tiled=True),
    )
    preactivation_rows = jnp.dot(flat_in, full_up, preferred_element_type=jnp.float32)
    hidden = gelu_tanh(preactivation_rows).astype(jnp.bfloat16)
    partial_value = jnp.dot(hidden, full_down, preferred_element_type=jnp.float32)
    branch = (
        lax.psum(partial_value.astype(jnp.bfloat16), "mp")
        .astype(jnp.float32)
        .reshape(batch, length, width)
    )
    block_out = (joined32 + gate_mod * branch).astype(jnp.bfloat16)
    d_out32 = d_output.astype(jnp.float32)
    d_branch = (d_out32 * gate_mod).astype(jnp.bfloat16).reshape(batch * length, width)
    hidden_gradient = contract_cols(d_branch, full_down)
    _, gelu_back = jax.vjp(gelu_tanh, preactivation_rows)
    d_pre = gelu_back(hidden_gradient)[0].astype(jnp.bfloat16)
    d_part = contract_cols(d_pre, full_up)
    d_mod = lax.psum(d_part.astype(jnp.bfloat16), "mp").astype(jnp.float32)
    owned_mod, owned_branch = (
        lax.all_to_all(flat_in, "dp", split_axis=1, concat_axis=0, tiled=True),
        lax.all_to_all(d_branch, "dp", split_axis=1, concat_axis=0, tiled=True),
    )
    grad_up = contract_rows(owned_mod, lax.all_gather(d_pre, "dp", axis=0, tiled=True))
    grad_down_t = contract_rows(owned_branch, lax.all_gather(hidden, "dp", axis=0, tiled=True))
    grad_down = grad_down_t.T
    d_normed = d_mod.reshape(batch, length, width) * (1.0 + scale_mod)
    d_full = d_out32 + inv_std * (
        d_normed
        - jnp.mean(d_normed, axis=-1, keepdims=True)
        - normed * jnp.mean(d_normed * normed, axis=-1, keepdims=True)
    )
    text_len = null_prompt.shape[0]
    null_part = jnp.sum(
        jnp.where(dropped[:, None, None], d_full[:, :text_len], jnp.float32(0.0)), axis=0
    )
    grad_null = lax.psum(null_part.astype(jnp.bfloat16), "dp").astype(jnp.float32)
    return (block_out, d_full.astype(jnp.bfloat16), grad_up, grad_down, grad_null)


def solution(mesh):
    placed = (
        P("dp", None, None),
        P("dp", None, None),
        P(),
        P("dp"),
        P("dp"),
        P(),
        P("dp", "mp"),
        P("mp", "dp"),
        P("dp", None, None),
    )
    return jax.shard_map(
        shards,
        mesh=mesh,
        in_specs=placed,
        out_specs=(P("dp", None, None), P("dp", None, None), P("dp", "mp"), P("mp", "dp"), P()),
        check_vma=False,
    )
```

profile of v0, /device:TPU:0, one launch (start us, length us, event | category | flops | bytes accessed | tf_op | source)
XLA Modules:
  0.0 1318.2 jit_solution(9674357997162976993)
XLA Ops:
  7.2 0.0 copy-start
  7.2 0.0 copy-start.8
  7.2 0.0 copy-start.9
  7.2 0.0 copy-start.2
  7.2 0.0 all-gather.5.cloned.1.call-start
  7.3 0.7 all-gather.5.cloned.1.call-update
  7.9 0.0 all-gather.7.cloned.1.call-start
  8.0 0.7 all-gather.7.cloned.1.call-update
  8.7 0.0 all-reduce.6.cloned.1.call-start
  8.7 0.0 copy-start.4
  10.2 0.0 copy-done.8
  10.2 0.0 copy-done.9
  10.2 0.0 copy-done.2
  10.2 0.3 convert_reduce_fusion
  10.5 0.6 fusion.12
  11.1 0.0 copy-done
  11.1 0.5 fusion.36
  11.6 0.1 fusion.41
  11.7 0.0 copy-done.4
  11.7 1.5 fusion.13
  13.2 361.5 %all-gather.5.cloned.1.call-done = bf16[3072,3072]{1,0:T(8,128)(2,1)} async-done(((bf16[384,3072]{1,0:T(8,128)(2,1)}), bf16[3072,3072]{1,0:T(8,128)(2,1)}) %all-gather.5.cloned.1.call-update) | async-done | bytes 18874384 | tf_op jit(solution)/shard_map/all_gather | solution.py:55
  374.7 14.2 %multiply_convert_fusion = (bf16[256,3072]{1,0:T(8,128)(2,1)}, f32[256,3072]{1,0:T(8,128)}) fusion(bf16[3072,3072]{1,0:T(8,128)(2,1)} %all-gather.5.cloned.1.call-done, f32[3072]{0:T(1024)S(1)} %bitcast.82, f32[3072]{0:T(1024)S(1)} %bitcast.79, f32[256]{0:T(256)S(1)} %add_rsqrt_fusion, f32[256]{0:T(256)S(1)} %broadcast_multiply_fusion.2, ...), kind=kOutput, calls=%fused_computation.34 | convolution fusion | flops 4845993984 | bytes 25192448 | tf_op jit(solution)/shard_map/dot_general | solution.py:58
  388.9 349.8 %all-gather.7.cloned.1.call-done = bf16[3072,3072]{1,0:T(8,128)(2,1)} async-done(((bf16[3072,384]{1,0:T(8,128)(2,1)}), bf16[3072,3072]{1,0:T(8,128)(2,1)}) %all-gather.7.cloned.1.call-update) | async-done | bytes 18874384 | tf_op jit(solution)/shard_map/all_gather | solution.py:56
  738.7 12.3 fusion.20
  751.0 10.3 convolution_convert_fusion
  761.3 10.3 convolution_convert_fusion.1
  771.6 0.0 all-reduce.6.cloned.1.call-update
  771.6 0.0 all-reduce.4.cloned.1.call-start
  771.7 68.5 %all-reduce.6.cloned.1.call-done = (bf16[256,3072]{1,0:T(8,128)(2,1)}, bf16[256,3072]{1,0:T(8,128)(2,1)}) async-done(((bf16[256,3072]{1,0:T(8,128)(2,1)}, bf16[256,3072]{1,0:T(8,128)(2,1)}), (bf16[256,3072]{1,0:T(8,128)(2,1)}, bf16[256,3072]{1,0:T(8,128)(2,1)})) %all-reduce.6.cloned.1.call-update) | async-done | bytes 3145744 | tf_op jit(solution)/shard_map/psum | solution.py:62
  840.2 0.0 copy-start.5
  840.2 0.0 copy-start.6
  840.2 4.4 fusion.21
  844.6 0.0 copy-done.5
  844.6 0.0 copy-done.6
  844.6 1.6 convert_add_fusion
  846.3 0.0 copy-start.7
  846.3 1.1 copy-done.7
  847.4 0.8 fusion.34
  848.2 0.0 all-reduce.4.cloned.1.call-update
  848.2 0.0 all-gather.9.cloned.1.call-start
  848.3 0.5 all-gather.9.cloned.1.call-update
  848.8 0.0 all-gather.11.cloned.1.call-start
  848.9 0.5 all-gather.11.cloned.1.call-update
  849.5 0.2 copy.25
  849.7 2.5 add_convert_fusion
  852.3 0.0 copy-start.3
  852.3 1.3 copy.18
  853.6 5.5 all-to-all-start
  859.1 0.0 copy-done.3
  859.1 0.3 copy.26
  859.4 1.4 copy.19
  860.8 37.9 %all-to-all-done = bf16[256,8,384]{2,0,1:T(8,128)(2,1)} async-done(((bf16[256,8,384]{2,0,1:T(8,128)(2,1)}), bf16[256,8,384]{2,0,1:T(8,128)(2,1)}, u32[]{:S(2)}, u32[]{:S(2)}) %all-to-all-start) | async-done | bytes 1572896 | tf_op jit(solution)/shard_map/all_to_all | solution.py:75
  898.7 3.8 all-to-all-start.1
  902.4 44.3 %all-reduce.4.cloned.1.call-done = bf16[64,3072]{1,0:T(8,128)(2,1)} async-done(((bf16[64,3072]{1,0:T(8,128)(2,1)}), bf16[64,3072]{1,0:T(8,128)(2,1)}) %all-reduce.4.cloned.1.call-update) | async-done | bytes 393232 | tf_op jit(solution)/shard_map/psum | solution.py:91
  946.7 1.9 convert_element_type.92
  948.7 175.1 %all-gather.9.cloned.1.call-done = bf16[2048,3072]{1,0:T(8,128)(2,1)} async-done(((bf16[256,3072]{1,0:T(8,128)(2,1)}), bf16[2048,3072]{1,0:T(8,128)(2,1)}) %all-gather.9.cloned.1.call-update) | async-done | bytes 12582928 | tf_op jit(solution)/shard_map/all_gather | solution.py:78
  1123.7 9.9 fusion.43
  1133.7 0.0 all-to-all-done.1
  1133.7 166.4 %all-gather.11.cloned.1.call-done = bf16[2048,3072]{1,0:T(8,128)(2,1)} async-done(((bf16[256,3072]{1,0:T(8,128)(2,1)}), bf16[2048,3072]{1,0:T(8,128)(2,1)}) %all-gather.11.cloned.1.call-update) | async-done | bytes 12582928 | tf_op jit(solution)/shard_map/all_gather | solution.py:79
  1300.1 0.0 copy-start.1
  1300.1 11.2 fusion.44
  1311.3 0.0 copy-done.1
  (8 shorter events, 0.1 us)
Async XLA Ops:
  7.2 4.0 copy-start
  7.2 3.0 copy-start.8
  7.2 3.0 copy-start.9
  7.2 3.0 copy-start.2
  7.2 367.5 %all-gather.5.cloned.1.call-start = ((), (), s32[]{:S(2)}) async-start(), calls=%async_computation.2 | async-start | bytes 21233664 | tf_op jit(solution)/shard_map/all_gather | solution.py:55
  7.9 730.7 %all-gather.7.cloned.1.call-start = ((), (), s32[]{:S(2)}) async-start(), calls=%async_computation.3 | async-start | bytes 21233664 | tf_op jit(solution)/shard_map/all_gather | solution.py:56
  8.7 831.5 %all-reduce.6.cloned.1.call-start = ((), (), s32[]{:S(2)}) async-start(), calls=%async_computation.7 | async-start | bytes 6291456 | tf_op jit(solution)/shard_map/psum | solution.py:62
  8.7 3.0 copy-start.4
  771.6 175.1 %all-reduce.4.cloned.1.call-start = ((), (), s32[]{:S(2)}) async-start(), calls=%async_computation.6 | async-start | bytes 786432 | tf_op jit(solution)/shard_map/psum | solution.py:91
  840.2 4.4 copy-start.5
  840.2 4.4 copy-start.6
  846.3 1.1 copy-start.7
  848.2 275.5 %all-gather.9.cloned.1.call-start = ((), (), s32[]{:S(2)}) async-start(), calls=%async_computation.4 | async-start | bytes 14155776 | tf_op jit(solution)/shard_map/all_gather | solution.py:78
  848.8 451.3 %all-gather.11.cloned.1.call-start = ((), (), s32[]{:S(2)}) async-start(), calls=%async_computation.5 | async-start | bytes 14155776 | tf_op jit(solution)/shard_map/all_gather | solution.py:79
  852.3 6.9 copy-start.3
  853.6 45.0 %all-to-all-start = ((bf16[256,8,384]{2,0,1:T(8,128)(2,1)}), bf16[256,8,384]{2,0,1:T(8,128)(2,1)}, u32[]{:S(2)}, u32[]{:S(2)}) async-start(bf16[256,8,384]{2,0,1:T(8,128)(2,1)} %copy.18), calls=%async_computation | async-start | bytes 3145728 | tf_op jit(solution)/shard_map/all_to_all | solution.py:75
  898.7 235.0 %all-to-all-start.1 = ((bf16[256,8,384]{2,0,1:T(8,128)(2,1)}), bf16[256,8,384]{2,0,1:T(8,128)(2,1)S(1)}, u32[]{:S(2)}, u32[]{:S(2)}) async-start(bf16[256,8,384]{2,0,1:T(8,128)(2,1)} %copy.19), calls=%async_computation.1 | async-start | bytes 3145728 | tf_op jit(solution)/shard_map/all_to_all | solution.py:76
  1300.1 11.2 copy-start.1
Sparse Core Ops, SparseCore 0:
  9.6 365.1 all-gather.4
  376.3 362.3 all-gather.6
  771.7 68.4 all-reduce.5
  848.4 98.3 all-reduce.3
  948.8 174.9 all-gather.8
  1125.8 174.2 all-gather.10
where the time goes:
time: 1320 us
  waiting for transfers between devices  1210 us (92%)
  matrix products  68.8 us (5%)
  between operations  15.7 us (1%)
  other arithmetic  13.8 us (1%)
    all_gather x1, waiting for transfers between devices, shards(): lax.all_gather(w_up, 'dp', axis=0, tiled=True)  362 us
    all_gather x1, waiting for transfers between devices, shards(): lax.all_gather(w_down, 'dp', axis=1, tiled=True)  350 us
    all_gather x1, waiting for transfers between devices, shards(): lax.all_gather(d_pre, 'dp', axis=0, tiled=True)  175 us
    all_gather x1, waiting for transfers between devices, shards(): lax.all_gather(hidden, 'dp', axis=0, tiled=True)  166 us
    psum x1, waiting for transfers between devices, shards(): lax.psum(partial_value.astype(jnp.bfloat16), 'mp').astype(jnp.float32)  68.5 us
    psum x1, waiting for transfers between devices, shards(): lax.psum(null_part.astype(jnp.bfloat16), 'dp').astype(jnp.float32)  44.3 us
    all_to_all x1, waiting for transfers between devices, shards(): lax.all_to_all(flat_in, 'dp', split_axis=1, concat_axis=0, tiled=True)  37.9 us
  transfers between devices with their start and end apart: 8, of which 7 were waited for; matrix products, arithmetic and copies ran while one was open for 3% of the time, Pallas kernels for 0%

commit v1 on v0

--- a/solution.py
+++ b/solution.py
@@ -59,7 +59,7 @@
     hidden = gelu_tanh(preactivation_rows).astype(jnp.bfloat16)
     partial_value = jnp.dot(hidden, full_down, preferred_element_type=jnp.float32)
     branch = (
-        lax.psum(partial_value.astype(jnp.bfloat16), "mp")
+        jnp.sum(lax.all_gather(partial_value.astype(jnp.bfloat16), "mp"), axis=0)
         .astype(jnp.float32)
         .reshape(batch, length, width)
     )

time: 1320 us -> 1350 us (1.023)
    all_gather x0 -> x1, waiting for transfers between devices: none -> 46.2 us  [shards(): lax.all_gather(partial_value.astype(jnp.bfloat16), 'mp')]
    all_to_all x1, waiting for transfers between devices: 37.9 us -> 0.01 us  [shards(): lax.all_to_all(flat_in, 'dp', split_axis=1, concat_axis=0, tiled=True)]
    all_to_all x1, waiting for transfers between devices: 0.01 us -> 34.8 us  [shards(): lax.all_to_all(d_branch, 'dp', split_axis=1, concat_axis=0, tiled=True)]
    psum x1, waiting for transfers between devices: 68.5 us -> 43 us  [shards(): d_mod = lax.psum(d_part.astype(jnp.bfloat16), 'mp').astype(jnp.float32)]
  transfers between devices with their start and end apart: 8 -> 9, of which waited for: 7 -> 8; matrix products, arithmetic and copies ran while one was open for 3% -> 3% of each run, Pallas kernels for 0% -> 0%
where the time goes in v1:
time: 1350 us
  waiting for transfers between devices  1220 us (90%)
  matrix products  68.8 us (5%)
  other arithmetic  21.5 us (2%)
  between operations  15.6 us (1%)
    all_gather x1, waiting for transfers between devices, shards(): lax.all_gather(w_up, 'dp', axis=0, tiled=True)  363 us
    all_gather x1, waiting for transfers between devices, shards(): lax.all_gather(w_down, 'dp', axis=1, tiled=True)  350 us
    all_gather x1, waiting for transfers between devices, shards(): lax.all_gather(hidden, 'dp', axis=0, tiled=True)  176 us
    all_gather x1, waiting for transfers between devices, shards(): lax.all_gather(d_pre, 'dp', axis=0, tiled=True)  165 us
    all_gather x1, waiting for transfers between devices, shards(): lax.all_gather(partial_value.astype(jnp.bfloat16), 'mp')  46.2 us
    psum x1, waiting for transfers between devices, shards(): lax.psum(null_part.astype(jnp.bfloat16), 'dp').astype(jnp.float32)  43.7 us
    psum x1, waiting for transfers between devices, shards(): d_mod = lax.psum(d_part.astype(jnp.bfloat16), 'mp').astype(jnp.float32)  43 us
    all_to_all x1, waiting for transfers between devices, shards(): lax.all_to_all(d_branch, 'dp', split_axis=1, concat_axis=0, tiled=True)  34.8 us
  transfers between devices with their start and end apart: 9, of which 8 were waited for; matrix products, arithmetic and copies ran while one was open for 3% of the time, Pallas kernels for 0%

profile of v1, /device:TPU:0, one launch (start us, length us, event | category | flops | bytes accessed | tf_op | source)
XLA Modules:
  0.0 1347.7 jit_solution(9799871473807547904)
XLA Ops:
  7.2 0.0 copy-start
  7.2 0.0 copy-start.6
  7.2 0.0 copy-start.7
  7.2 0.0 copy-start.2
  7.2 0.0 all-gather.7.cloned.1.call-start
  7.3 0.7 all-gather.7.cloned.1.call-update
  7.9 0.0 all-gather.9.cloned.1.call-start
  8.0 0.7 all-gather.9.cloned.1.call-update
  8.7 0.0 all-gather.15.cloned.1.call-start
  10.0 0.0 copy-done.6
  10.0 0.0 copy-done.7
  10.1 0.0 copy-done.2
  10.1 0.3 convert_reduce_fusion
  10.4 0.6 fusion.9
  11.0 0.0 copy-done
  11.0 0.5 fusion.24
  11.5 0.1 fusion.30
  11.6 363.1 %all-gather.7.cloned.1.call-done = bf16[3072,3072]{1,0:T(8,128)(2,1)} async-done(((bf16[384,3072]{1,0:T(8,128)(2,1)}), bf16[3072,3072]{1,0:T(8,128)(2,1)}) %all-gather.7.cloned.1.call-update) | async-done | bytes 18874384 | tf_op jit(solution)/shard_map/all_gather | solution.py:55
  374.7 14.2 %multiply_convert_fusion = (bf16[256,3072]{1,0:T(8,128)(2,1)}, f32[256,3072]{1,0:T(8,128)}) fusion(bf16[3072,3072]{1,0:T(8,128)(2,1)} %all-gather.7.cloned.1.call-done, f32[3072]{0:T(1024)S(1)} %bitcast.82, f32[3072]{0:T(1024)S(1)} %bitcast.78, f32[256]{0:T(256)S(1)} %add_rsqrt_fusion, f32[256]{0:T(256)S(1)} %broadcast_multiply_fusion.2, ...), kind=kOutput, calls=%fused_computation.25 | convolution fusion | flops 4845993984 | bytes 25192448 | tf_op jit(solution)/shard_map/dot_general | solution.py:58
  388.9 349.8 %all-gather.9.cloned.1.call-done = bf16[3072,3072]{1,0:T(8,128)(2,1)} async-done(((bf16[3072,384]{1,0:T(8,128)(2,1)}), bf16[3072,3072]{1,0:T(8,128)(2,1)}) %all-gather.9.cloned.1.call-update) | async-done | bytes 18874384 | tf_op jit(solution)/shard_map/all_gather | solution.py:56
  738.7 10.3 convolution_convert_fusion.1
  749.0 0.0 all-gather.15.cloned.1.call-update
  749.0 0.2 all-reduce.3.cloned.1.call-start
  749.2 46.2 %all-gather.15.cloned.1.call-done = bf16[1024,3072]{1,0:T(8,128)(2,1)} async-done(((bf16[256,3072]{1,0:T(8,128)(2,1)}), bf16[1024,3072]{1,0:T(8,128)(2,1)}) %all-gather.15.cloned.1.call-update) | async-done | bytes 6291472 | tf_op jit(solution)/shard_map/all_gather | solution.py:62
  795.5 5.5 reduce_sum.54
  801.0 0.0 copy-start.8
  801.0 4.0 fusion
  805.0 0.0 copy-start.3
  805.0 1.2 copy-done.3
  806.1 0.0 copy-done.8
  806.1 11.6 fusion.7
  817.7 10.3 convolution_convert_fusion
  828.0 0.0 all-reduce.3.cloned.1.call-update
  828.0 0.0 all-reduce.5.cloned.1.call-start
  828.1 43.0 %all-reduce.3.cloned.1.call-done = bf16[256,3072]{1,0:T(8,128)(2,1)} async-done(((bf16[256,3072]{1,0:T(8,128)(2,1)}), bf16[256,3072]{1,0:T(8,128)(2,1)}) %all-reduce.3.cloned.1.call-update) | async-done | bytes 1572880 | tf_op jit(solution)/shard_map/psum | solution.py:73
  871.0 0.0 copy-start.4
  871.0 2.5 fusion.11
  873.5 0.0 copy-done.4
  873.5 3.0 convert_add_fusion.1
  876.6 0.0 copy-start.5
  876.6 1.1 copy-done.5
  877.7 0.8 fusion.22
  878.5 0.0 all-reduce.5.cloned.1.call-update
  878.5 0.0 all-gather.13.cloned.1.call-start
  878.6 0.5 all-gather.13.cloned.1.call-update
  879.1 0.0 all-gather.11.cloned.1.call-start
  879.2 0.7 all-gather.11.cloned.1.call-update
  879.9 1.7 copy.26
  881.6 1.3 copy.19
  882.9 5.5 all-to-all-start.1
  888.4 1.2 copy.25
  889.7 2.7 add_convert_fusion
  892.5 1.3 copy.18
  893.8 34.8 %all-to-all-done.1 = bf16[256,8,384]{2,0,1:T(8,128)(2,1)} async-done(((bf16[256,8,384]{2,0,1:T(8,128)(2,1)}), bf16[256,8,384]{2,0,1:T(8,128)(2,1)}, u32[]{:S(2)}, u32[]{:S(2)}) %all-to-all-start.1) | async-done | bytes 1572896 | tf_op jit(solution)/shard_map/all_to_all | solution.py:76
  928.6 3.8 all-to-all-start
  932.4 43.7 %all-reduce.5.cloned.1.call-done = bf16[64,3072]{1,0:T(8,128)(2,1)} async-done(((bf16[64,3072]{1,0:T(8,128)(2,1)}), bf16[64,3072]{1,0:T(8,128)(2,1)}) %all-reduce.5.cloned.1.call-update) | async-done | bytes 393232 | tf_op jit(solution)/shard_map/psum | solution.py:91
  976.0 1.9 convert_element_type.113
  978.0 176.0 %all-gather.13.cloned.1.call-done = bf16[2048,3072]{1,0:T(8,128)(2,1)} async-done(((bf16[256,3072]{1,0:T(8,128)(2,1)}), bf16[2048,3072]{1,0:T(8,128)(2,1)}) %all-gather.13.cloned.1.call-update) | async-done | bytes 12582928 | tf_op jit(solution)/shard_map/all_gather | solution.py:79
  1153.9 11.6 fusion.33
  1165.5 0.0 all-to-all-done
  1165.5 164.9 %all-gather.11.cloned.1.call-done = bf16[2048,3072]{1,0:T(8,128)(2,1)} async-done(((bf16[256,3072]{1,0:T(8,128)(2,1)}), bf16[2048,3072]{1,0:T(8,128)(2,1)}) %all-gather.11.cloned.1.call-update) | async-done | bytes 12582928 | tf_op jit(solution)/shard_map/all_gather | solution.py:78
  1330.4 0.0 copy-start.1
  1330.4 10.4 fusion.32
  1340.8 0.0 copy-done.1
  (8 shorter events, 0.1 us)
Async XLA Ops:
  7.2 3.8 copy-start
  7.2 2.9 copy-start.6
  7.2 2.9 copy-start.7
  7.2 2.9 copy-start.2
  7.2 367.5 %all-gather.7.cloned.1.call-start = ((), (), s32[]{:S(2)}) async-start(), calls=%async_computation.2 | async-start | bytes 21233664 | tf_op jit(solution)/shard_map/all_gather | solution.py:55
  7.9 730.7 %all-gather.9.cloned.1.call-start = ((), (), s32[]{:S(2)}) async-start(), calls=%async_computation.3 | async-start | bytes 21233664 | tf_op jit(solution)/shard_map/all_gather | solution.py:56
  8.7 786.8 %all-gather.15.cloned.1.call-start = ((), (), s32[]{:S(2)}) async-start(), calls=%async_computation.8 | async-start | bytes 7864320 | tf_op jit(solution)/shard_map/all_gather | solution.py:62
  749.0 122.1 %all-reduce.3.cloned.1.call-start = ((), (), s32[]{:S(2)}) async-start(), calls=%async_computation.4 | async-start | bytes 3145728 | tf_op jit(solution)/shard_map/psum | solution.py:73
  801.0 5.2 copy-start.8
  805.0 1.2 copy-start.3
  828.0 148.0 %all-reduce.5.cloned.1.call-start = ((), (), s32[]{:S(2)}) async-start(), calls=%async_computation.7 | async-start | bytes 786432 | tf_op jit(solution)/shard_map/psum | solution.py:91
  871.0 2.5 copy-start.4
  876.6 1.1 copy-start.5
  878.5 275.4 %all-gather.13.cloned.1.call-start = ((), (), s32[]{:S(2)}) async-start(), calls=%async_computation.6 | async-start | bytes 14155776 | tf_op jit(solution)/shard_map/all_gather | solution.py:79
  879.1 451.3 %all-gather.11.cloned.1.call-start = ((), (), s32[]{:S(2)}) async-start(), calls=%async_computation.5 | async-start | bytes 14155776 | tf_op jit(solution)/shard_map/all_gather | solution.py:78
  882.9 45.7 %all-to-all-start.1 = ((bf16[256,8,384]{2,0,1:T(8,128)(2,1)}), bf16[256,8,384]{2,0,1:T(8,128)(2,1)}, u32[]{:S(2)}, u32[]{:S(2)}) async-start(bf16[256,8,384]{2,0,1:T(8,128)(2,1)} %copy.19), calls=%async_computation.1 | async-start | bytes 3145728 | tf_op jit(solution)/shard_map/all_to_all | solution.py:76
  928.6 236.9 %all-to-all-start = ((bf16[256,8,384]{2,0,1:T(8,128)(2,1)}), bf16[256,8,384]{2,0,1:T(8,128)(2,1)S(1)}, u32[]{:S(2)}, u32[]{:S(2)}) async-start(bf16[256,8,384]{2,0,1:T(8,128)(2,1)} %copy.18), calls=%async_computation | async-start | bytes 3145728 | tf_op jit(solution)/shard_map/all_to_all | solution.py:75
  1330.4 10.4 copy-start.1
Sparse Core Ops, SparseCore 0:
  9.6 365.1 all-gather.6
  376.3 362.3 all-gather.8
  749.1 46.3 all-gather.14
  828.1 42.8 all-reduce.2
  878.7 97.3 all-reduce.4
  978.7 175.2 all-gather.12
  1156.1 174.2 all-gather.10
